TPU v7x, 32 devices: a whole 2x2x4 slice. The times are simulated.
32 devices in a mesh: seq: 8 (over z, y), head: 4 (over x, core).
Axes of the slice: x: 2, y: 2, z: 4, core: 2. Of those that a mesh axis runs over, the one named last changes fastest.
Arguments:
- inputs: bfloat16 [2048, 5120], P('seq', 'head'), may hold values from -6 to 6
- time_step: float32 [80, 2048], P('head', 'seq'), may hold values from 0.01 to 0.3
- decay_rate: float32 [80], P('head'), may hold values from 0.0001 to 1
- input_map: bfloat16 [2048, 128], P('seq'), may hold values from -6 to 6
- output_map: bfloat16 [2048, 128], P('seq'), may hold values from -0.59765625 to 0.59765625
- output_grad: bfloat16 [2048, 5120], P('seq', 'head'), may hold values from -3 to 3
- span_states: float32 [8, 80, 64, 128], P('seq', 'head'), may hold values from -6 to 6
- resets: int32 [8], P('seq'), may hold values from 0 to 4095
Outputs:
- grad_inputs: bfloat16 [2048, 5120], P('seq', 'head')
- grad_input_map: float32 [2048, 128], P('seq')
- grad_rate: float32 [80], P('head')
Inputs may be any that keep to these rules, and one draw needn't show every extreme that they name: `resets`: A value p under 256 means that a document starts at position p of that span; a value of 256 or more means that none starts in it.
All inputs are finite; a program needn't handle non-finite values.
Results may differ from a plain program's by a relative error of at most 0.003.
Values sent between devices are 32-bit elements; how exact they have to be, the bound alone decides.
A program may use at most 64 MiB of HBM per device.

v0:
```python
import jax
import jax.numpy as jnp
from jax import lax
from jax.sharding import PartitionSpec as P

highest = lax.Precision.HIGHEST


def prepare(x_block, step_block, decay_rate, b_block, c_block, grad_block, start_state, reset_at):
    block_len = step_block.shape[1]
    positions = jnp.arange(block_len, dtype=jnp.int32)
    later_doc = positions >= reset_at
    no_reset = reset_at >= block_len
    elapsed = jnp.cumsum(step_block, axis=1)
    log_decay = -decay_rate[:, None] * elapsed
    joined = (later_doc[:, None] == later_doc[None, :]) & (positions[None, :] >= positions[:, None])
    log_gaps = log_decay[:, None, :] - log_decay[:, :, None]
    pair_weight = jnp.where(joined[None], jnp.exp(jnp.where(joined[None], log_gaps, 0.0)), 0.0)
    intersection = jnp.dot(b_block, c_block.T, preferred_element_type=jnp.float32)
    products = jnp.einsum("shp,uhp->hsu", x_block, grad_block, preferred_element_type=jnp.float32)
    mixing = (pair_weight * intersection[None]).astype(jnp.bfloat16)
    pair_terms = pair_weight * products
    paired = pair_terms.astype(jnp.bfloat16)
    dx_inner = jnp.einsum("hsu,uhp->shp", mixing, grad_block, preferred_element_type=jnp.float32)
    db_inner = jnp.einsum("hsu,un->hsn", paired, c_block, preferred_element_type=jnp.float32)
    start_weight = jnp.where(later_doc[None], 0.0, jnp.exp(log_decay))
    end_weight = jnp.where(
        (later_doc | no_reset)[None], jnp.exp(log_decay[:, -1:] - log_decay), 0.0
    )
    carry_gain = jnp.where(no_reset, jnp.exp(log_decay[:, -1]), 0.0)
    c_wide = c_block.astype(jnp.float32)
    grad_wide = grad_block.astype(jnp.float32)
    weighted_c = start_weight[:, :, None] * c_wide[None]
    boundary_grad = jnp.einsum("hun,uhp->hpn", weighted_c, grad_wide, precision=highest)
    state_read = jnp.einsum("uhp,hpn->hun", grad_wide, start_state, precision=highest)
    start_term = jnp.sum(state_read * c_wide[None], axis=2)
    inside_term = jnp.sum(
        pair_terms
        * intersection[None]
        * step_block[:, :, None]
        * (elapsed[:, None, :] - elapsed[:, :, None]),
        axis=(1, 2),
    )
    entry_term = jnp.sum(start_weight * elapsed * start_term, axis=1)
    return (
        carry_gain,
        boundary_grad,
        dx_inner,
        db_inner,
        inside_term + entry_term,
        end_weight,
        elapsed,
    )


def finish(prepared, x_block, step_block, b_block, start_state, carried):
    carry_gain, boundary_grad, dx_inner, db_inner, partial_rate, end_weight, elapsed = prepared
    b_wide = b_block.astype(jnp.float32)
    x_wide = x_block.astype(jnp.float32)
    carried_b = jnp.einsum("sn,hpn->shp", b_wide, carried, precision=highest)
    carried_x = jnp.einsum("shp,hpn->hsn", x_wide, carried, precision=highest)
    step_rows = step_block.T[:, :, None]
    end_rows = end_weight.T[:, :, None]
    grad_x = (step_rows * (dx_inner + end_rows * carried_b)).astype(jnp.bfloat16)
    grad_b = jnp.sum(
        step_block[:, :, None] * (db_inner + end_weight[:, :, None] * carried_x), axis=0
    )
    last_elapsed = elapsed[:, -1]
    leaving_term = jnp.sum(
        end_weight
        * step_block
        * (last_elapsed[:, None] - elapsed)
        * jnp.sum(carried_x * b_wide[None], axis=2),
        axis=1,
    )
    through_term = carry_gain * last_elapsed * jnp.sum(carried * start_state, axis=(1, 2))
    return (grad_x, grad_b, partial_rate + leaving_term + through_term)


def backward_step(running, members):
    grad_piece, gain_piece = members
    return (grad_piece + gain_piece[:, None] * running, running)


def body(inputs, time_step, decay_rate, input_map, output_map, output_grad, span_states, resets):
    length = time_step.shape[1]
    block_count = span_states.shape[0]
    block_len = length // block_count
    head_count = decay_rate.shape[0]
    head_width = inputs.shape[1] // head_count
    number = 0
    x_block = inputs.reshape(block_len, head_count, head_width)
    grad_block = output_grad.reshape(block_len, head_count, head_width)
    step_block = time_step
    b_block = input_map
    prepared = prepare(
        x_block,
        step_block,
        decay_rate,
        b_block,
        output_map,
        grad_block,
        span_states[number],
        resets[number],
    )
    pieces = [(prepared, x_block, step_block, b_block)]
    gain_total = jnp.ones((head_count,), jnp.float32)
    grad_total = jnp.zeros_like(span_states[0])
    for number in reversed(range(block_count)):
        gain_block, grad_block_sum = (pieces[number][0][0], pieces[number][0][1])
        grad_total = grad_block_sum + gain_block[:, None, None] * grad_total
        gain_total = gain_block * gain_total
    seq_count = lax.axis_size("seq")
    entries = grad_total.shape[1] * grad_total.shape[2]
    sliced = grad_total.reshape(head_count, seq_count, entries // seq_count)
    received = lax.all_to_all(sliced, "seq", split_axis=1, concat_axis=1, tiled=True)
    gains = lax.all_gather(gain_total[None], "seq", axis=0, tiled=True)
    ending, exclusive = lax.scan(
        backward_step,
        jnp.zeros_like(received[:, 0]),
        (jnp.transpose(received, (1, 0, 2)), gains),
        reverse=True,
    )
    returned = lax.all_to_all(
        jnp.transpose(exclusive, (1, 0, 2)), "seq", split_axis=1, concat_axis=1, tiled=True
    )
    incoming = returned.reshape(grad_total.shape)
    carried = incoming
    grad_x_list = [None] * block_count
    grad_b_list = [None] * block_count
    rate_total = jnp.zeros((head_count,), jnp.float32)
    for number in reversed(range(block_count)):
        prepared, x_block, step_block, b_block = pieces[number]
        grad_x, grad_b, rate_part = finish(
            prepared, x_block, step_block, b_block, span_states[number], carried
        )
        grad_x_list[number] = grad_x.reshape(block_len, head_count * head_width)
        grad_b_list[number] = grad_b
        rate_total = rate_part
        carried = prepared[1] + prepared[0][:, None, None] * carried
    grad_inputs = grad_x_list[0]
    grad_input_map = lax.psum(grad_b_list[0], "head")
    grad_rate = -lax.psum(rate_total, "seq")
    return (grad_inputs, grad_input_map, grad_rate)


def solution(mesh):
    in_specs = (
        P("seq", "head"),
        P("head", "seq"),
        P("head"),
        P("seq", None),
        P("seq", None),
        P("seq", "head"),
        P("seq", "head", None, None),
        P("seq"),
    )
    out_specs = (P("seq", "head"), P("seq", None), P("head"))
    return jax.shard_map(body, mesh=mesh, in_specs=in_specs, out_specs=out_specs, check_vma=False)
```

profile of v0, /device:TPU:0, one launch (start us, length us, event | category | flops | bytes accessed | tf_op | source)
XLA Modules:
  0.0 141.0 jit_solution(17333116644024165966)
XLA Ops:
  8.6 0.8 reshape.290
  11.2 0.9 copy.37
  12.2 1.4 copy.36
  13.6 1.7 %fusion.31 = f32[20,64,128]{2,1,0:T(8,128)S(1)} fusion(bf16[256,20,64]{0,2,1:T(8,128)(2,1)S(1)} %bitcast.80, f32[256,128]{0,1:T(8,128)S(1)} %copy.37, f32[20,256]{1,0:T(8,128)S(1)} %get-tuple-element.152, f32[20]{0:T(128)S(1)} %broadcast_multiply_fusion.1), kind=kOutput, calls=%fused_computation.38 | convolution fusion | flops 504135680 | bytes 1462352 | tf_op jit(solution)/shard_map/hun,uhp->hpn/dot_general | solution.py:34
  15.4 1.3 copy.39
  16.7 7.3 %all-to-all-start = ((f32[20,8,1024]{2,0,1:T(8,128)}), f32[20,8,1024]{2,0,1:T(8,128)S(1)}, u32[]{:S(2)}, u32[]{:S(2)}) async-start(f32[20,8,1024]{2,0,1:T(8,128)} %copy.39), calls=%async_computation | async-start | bytes 1572864 | tf_op jit(solution)/shard_map/all_to_all | solution.py:116
  25.6 26.1 %all-reduce = f32[160]{0:T(256)S(1)} all-reduce(f32[160]{0:T(256)S(1)} %dynamic-update-slice), channel_id=2, replica_groups=mesh['seq'=8,'head'=4] {'seq'}, use_global_device_ids=true, to_apply=%add | all-reduce | flops 160 | bytes 1280
  53.9 0.7 slice_reduce_fusion.1
  54.7 1.4 %fusion.37 = pred[256,256]{1,0:T(8,128)(4,1)} fusion(pred[256]{0:T(512)(128)(4,1)} %copy-done.10), kind=kLoop, calls=%fused_computation.42 | loop fusion | flops 196608 | bytes 65792 | tf_op jit(solution)/shard_map/and | solution.py:16
  56.1 1.8 %fusion.43 = f32[256,256]{1,0:T(8,128)} fusion(bf16[256,128]{1,0:T(8,128)(2,1)} %param.13, bf16[256,128]{1,0:T(8,128)(2,1)} %param.14), kind=kOutput, calls=%fused_computation.64 | convolution fusion | flops 16777216 | bytes 393216 | tf_op jit(solution)/shard_map/dot_general | solution.py:19
  57.9 1.0 broadcast_in_dim.97
  58.9 11.4 %while.17 = (s32[]{:T(128)}, f32[20,1024]{1,0:T(8,128)S(1)}, f32[8,20,1024]{2,1,0:T(8,128)}, f32[8,20,1024]{2,1,0:T(8,128)S(1)}, f32[8,20]{1,0:T(8,128)}, /*index=5*/s32[]{:T(128)}, s32[]{:T(128)}, s32[]{:T(128)}) while((s32[]{:T(128)}, f32[20,1024]{1,0:T(8,128)S(1)}, f32[8,20,1024]{2,1,0:T(8,128)}, f32[8,20,1024]{2,1,0:T(8,128)S(1)}, ...), condition=%wide.region_3.4_spmd.clone, body=%wide.region_2.3_spmd.clone.sunk | while | flops 81924 | bytes 426352 | solution.py:118
  70.3 4.5 %all-to-all-start.1 = ((f32[20,8,1024]{2,0,1:T(8,128)}), f32[20,8,1024]{2,0,1:T(8,128)S(1)}, u32[]{:S(2)}, u32[]{:S(2)}) async-start(f32[20,8,1024]{2,0,1:T(8,128)} %bitcast.8), calls=%async_computation.1 | async-start | bytes 1572864 | tf_op jit(solution)/shard_map/all_to_all | solution.py:124
  74.8 2.8 %multiply_reduce_fusion.1 = f32[20,256]{1,0:T(8,128)} fusion(bf16[256,20,64]{0,2,1:T(8,128)(2,1)S(1)} %bitcast.81, f32[256,128]{0,1:T(8,128)} %copy-done.7, f32[1,20,64,128]{3,2,1,0:T(8,128)S(1)} %copy-done.2), kind=kOutput, calls=%fused_computation.17 | convolution fusion | flops 504622080 | bytes 1462272 | tf_op jit(solution)/shard_map/uhp,hpn->hun/dot_general | solution.py:35
  77.7 3.7 %fusion.21 = f32[256,20,64]{0,2,1:T(8,128)} fusion(bf16[256,20,64]{0,2,1:T(8,128)(2,1)S(1)} %bitcast.82, f32[256,256]{1,0:T(8,128)} %fusion.43, f32[20,256]{1,0:T(8,128)S(1)} %get-tuple-element.153, pred[256,256]{1,0:T(8,128)(4,1)} %fusion.37), kind=kOutput, calls=%fused_computation.29 | convolution fusion | flops 174325760 | bytes 2314240 | tf_op jit(solution)/shard_map/hsu,uhp->shp/dot_general | solution.py:24
  81.4 5.3 %multiply_reduce_fusion = (f32[20]{0:T(128)}, f32[20,256,256]{2,1,0:T(8,128)}) fusion(f32[20,256]{1,0:T(8,128)S(1)} %bitcast.86, f32[20,256]{1,0:T(8,128)S(1)} %copy-done.6, f32[256,256]{1,0:T(8,128)S(1)} %copy-done.5, f32[20,256]{1,0:T(8,128)S(1)} %get-tuple-element.153, pred[256,256]{1,0:T(8,128)(4,1)S(1)} %copy-done.8, ...), kind=kOutput, calls=%fused_computation.4 | convolution fusion | flops 179568624 | bytes 6942800 | tf_op jit(solution)/shard_map/shp,uhp->hsu/dot_general | solution.py:20
  86.8 5.5 %all-to-all-done.1 = f32[20,8,1024]{2,0,1:T(8,128)S(1)} async-done(((f32[20,8,1024]{2,0,1:T(8,128)}), f32[20,8,1024]{2,0,1:T(8,128)S(1)}, u32[]{:S(2)}, u32[]{:S(2)}) %all-to-all-start.1) | async-done | bytes 655392 | tf_op jit(solution)/shard_map/all_to_all | solution.py:124
  92.3 1.1 multiply_reduce_fusion.2
  93.4 2.8 %fusion.9 = (f32[20,256]{1,0:T(8,128)S(1)}, f32[20,128,256]{1,2,0:T(8,128)S(1)}) fusion(f32[256,128]{1,0:T(8,128)} %convert_element_type.21, f32[20,64,128]{2,1,0:T(8,128)S(1)} %reshape.294, bf16[256,20,64]{0,2,1:T(8,128)(2,1)S(1)} %bitcast.77), kind=kOutput, calls=%fused_computation.16 | convolution fusion | flops 504622080 | bytes 4083712 | tf_op jit(solution)/shard_map/shp,hpn->hsn/dot_general | solution.py:61
  96.5 5.2 %fusion.8 = f32[256,128]{1,0:T(8,128)} fusion(f32[20,128,256]{1,2,0:T(8,128)S(1)} %get-tuple-element.155, f32[20,256]{1,0:T(8,128)S(1)} %get-tuple-element.150, f32[20,256]{1,0:T(8,128)S(1)} %copy-done.6, f32[20,256,256]{2,1,0:T(8,128)} %get-tuple-element.157, f32[20,256]{1,0:T(8,128)S(1)} %get-tuple-element.153, pred[256,256]{1,0:T(8,128)(4,1)} %fusion.37, ...), kind=kOutput, calls=%fused_computation.15 | convolution fusion | flops 344686592 | bytes 8187904 | tf_op jit(solution)/shard_map/hsu,un->hsn/dot_general | solution.py:25
  102.4 19.4 %psum.15 = f32[20]{0:T(128)S(1)} all-reduce(f32[20]{0:T(128)S(1)} %multiply_add_fusion), channel_id=1, replica_groups=mesh['seq'=8,'head'=4] {'seq'}, use_global_device_ids=true, to_apply=%region_12.13 | all-reduce | flops 20 | bytes 160 | tf_op jit(solution)/shard_map/psum | solution.py:143
  121.8 1.1 copy.44
  123.4 9.1 %all-reduce.3.cloned.1.call-done = f32[256,128]{1,0:T(8,128)} async-done(((f32[256,128]{1,0:T(8,128)}), f32[256,128]{1,0:T(8,128)}) %all-reduce.3.cloned.1.call-update) | async-done | bytes 131088 | tf_op jit(solution)/shard_map/psum | solution.py:142
  132.6 1.6 %copy.62 = f32[256,128]{1,0:T(8,128)} copy(f32[256,128]{1,0:T(8,128)} %all-reduce.3.cloned.1.call-done) | data formatting | bytes 262144
  (98 shorter events, 18.6 us)
Async XLA Ops:
  7.2 16.8 %copy-start.20 = (u32[32]{0:T(128)S(1)}, u32[32]{0:T(128)}, u32[]{:S(2)}) copy-start(u32[32]{0:T(128)} %constant.57) | copy-start | bytes 388
  7.2 45.2 %copy-start.3 = (bf16[256,128]{1,0:T(8,128)(2,1)S(1)}, bf16[256,128]{1,0:T(8,128)(2,1)}, u32[]{:S(2)}) copy-start(bf16[256,128]{1,0:T(8,128)(2,1)} %param.13) | copy-start | bytes 196612
  7.2 45.8 %copy-start.1 = (bf16[256,1280]{1,0:T(8,128)(2,1)S(1)}, bf16[256,1280]{1,0:T(8,128)(2,1)}, u32[]{:S(2)}) copy-start(bf16[256,1280]{1,0:T(8,128)(2,1)} %param.10) | copy-start | bytes 1966084
  7.2 46.0 %copy-start.2 = (f32[1,20,64,128]{3,2,1,0:T(8,128)S(1)}, f32[1,20,64,128]{3,2,1,0:T(8,128)}, u32[]{:S(2)}) copy-start(f32[1,20,64,128]{3,2,1,0:T(8,128)} %param.16) | copy-start | bytes 1966084
  8.6 43.7 %copy-start.14 = (f32[20]{0:T(128)}, f32[20]{0:T(128)S(1)}, u32[]{:S(2)}) copy-start(f32[20]{0:T(128)S(1)} %neg.7) | copy-start | bytes 244
  10.9 41.4 %copy-start.10 = (pred[256]{0:T(512)(128)(4,1)}, pred[256]{0:T(512)(128)(4,1)S(1)}, u32[]{:S(2)}) copy-start(pred[256]{0:T(512)(128)(4,1)S(1)} %get-tuple-element.158) | copy-start | bytes 772
  11.2 41.1 %copy-start.11 = (f32[20]{0:T(128)}, f32[20]{0:T(128)S(1)}, u32[]{:S(2)}) copy-start(f32[20]{0:T(128)S(1)} %get-tuple-element.137) | copy-start | bytes 244
  12.2 1.4 copy-start.7
  16.7 41.2 %all-to-all-start = ((f32[20,8,1024]{2,0,1:T(8,128)}), f32[20,8,1024]{2,0,1:T(8,128)S(1)}, u32[]{:S(2)}, u32[]{:S(2)}) async-start(f32[20,8,1024]{2,0,1:T(8,128)} %copy.39), calls=%async_computation | async-start | bytes 1572864 | tf_op jit(solution)/shard_map/all_to_all | solution.py:116
  70.3 22.0 %all-to-all-start.1 = ((f32[20,8,1024]{2,0,1:T(8,128)}), f32[20,8,1024]{2,0,1:T(8,128)S(1)}, u32[]{:S(2)}, u32[]{:S(2)}) async-start(f32[20,8,1024]{2,0,1:T(8,128)} %bitcast.8), calls=%async_computation.1 | async-start | bytes 1572864 | tf_op jit(solution)/shard_map/all_to_all | solution.py:124
  74.8 57.8 %all-reduce.3.cloned.1.call-start = ((), (), s32[]{:S(2)}) async-start(), calls=%async_computation.2 | async-start | bytes 262144 | tf_op jit(solution)/shard_map/psum | solution.py:142
  77.7 3.7 %copy-start.5 = (f32[256,256]{1,0:T(8,128)S(1)}, f32[256,256]{1,0:T(8,128)}, u32[]{:S(2)}) copy-start(f32[256,256]{1,0:T(8,128)} %fusion.43) | copy-start | bytes 786436
  77.7 3.7 %copy-start.6 = (f32[20,256]{1,0:T(8,128)S(1)}, f32[20,256]{1,0:T(8,128)}, u32[]{:S(2)}) copy-start(f32[20,256]{1,0:T(8,128)} %param.11) | copy-start | bytes 61444
  77.7 3.7 %copy-start.8 = (pred[256,256]{1,0:T(8,128)(4,1)S(1)}, pred[256,256]{1,0:T(8,128)(4,1)}, u32[]{:S(2)}) copy-start(pred[256,256]{1,0:T(8,128)(4,1)} %fusion.37) | copy-start | bytes 196612
  86.8 9.4 %copy-start.9 = (f32[20,256]{1,0:T(8,128)S(1)}, f32[20,256]{1,0:T(8,128)}, u32[]{:S(2)}) copy-start(f32[20,256]{1,0:T(8,128)} %multiply_reduce_fusion.1) | copy-start | bytes 61444
  86.8 9.4 %copy-start.12 = (f32[20]{0:T(128)S(1)}, f32[20]{0:T(128)}, u32[]{:S(2)}) copy-start(f32[20]{0:T(128)} %copy-done.11) | copy-start | bytes 244
  86.8 9.5 %copy-start.13 = (f32[20]{0:T(128)S(1)}, f32[20]{0:T(128)}, u32[]{:S(2)}) copy-start(f32[20]{0:T(128)} %slice_reduce_fusion.1) | copy-start | bytes 244
  86.8 9.5 %copy-start.15 = (f32[20]{0:T(128)S(1)}, f32[20]{0:T(128)}, u32[]{:S(2)}) copy-start(f32[20]{0:T(128)} %copy-done.14) | copy-start | bytes 244
  86.8 9.5 %copy-start.16 = (pred[256]{0:T(512)(128)(4,1)S(1)}, pred[256]{0:T(512)(128)(4,1)}, u32[]{:S(2)}) copy-start(pred[256]{0:T(512)(128)(4,1)} %get-tuple-element.159) | copy-start | bytes 772
  86.8 9.5 %copy-start.18 = (pred[256]{0:T(512)(128)(4,1)S(1)}, pred[256]{0:T(512)(128)(4,1)}, u32[]{:S(2)}) copy-start(pred[256]{0:T(512)(128)(4,1)} %compare_bitcast_fusion) | copy-start | bytes 772
  96.5 5.2 %copy-start.17 = (f32[20]{0:T(128)S(1)}, f32[20]{0:T(128)}, u32[]{:S(2)}) copy-start(f32[20]{0:T(128)} %get-tuple-element.148) | copy-start | bytes 244
  96.5 5.2 %copy-start.19 = (f32[20]{0:T(128)S(1)}, f32[20]{0:T(128)}, u32[]{:S(2)}) copy-start(f32[20]{0:T(128)} %get-tuple-element.156) | copy-start | bytes 244
  96.5 5.2 %copy-start = (f32[256,20,64]{0,2,1:T(8,128)S(1)}, f32[256,20,64]{0,2,1:T(8,128)}, u32[]{:S(2)}) copy-start(f32[256,20,64]{0,2,1:T(8,128)} %fusion.21) | copy-start | bytes 3932164
  96.5 5.2 %copy-start.4 = (bf16[256,128]{1,0:T(8,128)(2,1)S(1)}, bf16[256,128]{1,0:T(8,128)(2,1)}, u32[]{:S(2)}) copy-start(bf16[256,128]{1,0:T(8,128)(2,1)} %param.13) | copy-start | bytes 196612
Sparse Core Ops, SparseCore 0:
  101.8 30.7 all-reduce.2
where the time goes:
time: 142 us; the launch traced here: 141 us
  blocking collectives  45.5 us (32%)
  matrix products  24 us (17%)
  local copies, waits for them, and re-layouts  16.6 us (12%)
  between operations  15.8 us (11%)
  waiting for transfers between devices  14.6 us (10%)
  other arithmetic  12.4 us (9%)
  starting transfers between devices  11.9 us (8%)
    unnamed x1, blocking collectives  26.1 us
    psum x1, blocking collectives, body(): grad_rate = -lax.psum(rate_total, 'seq')  19.4 us
    psum x1, waiting for transfers between devices, body(): grad_input_map = lax.psum(grad_b_list[0], 'head')  9.15 us
    all_to_all x1, starting transfers between devices, body(): lax.all_to_all(sliced, 'seq', split_axis=1, concat_axis=1, tiled=True)  7.31 us
    mul x8, local copies, waits for them, and re-layouts, backward_step(): return (grad_piece + gain_piece[:, None] * running, running)  5.48 us
    all_to_all x1, waiting for transfers between devices, body(): lax.all_to_all(jnp.transpose(exclusive, (1, 0, 2)), 'seq', split_axis=1,...  5.48 us
    dot_general x1, matrix products, prepare(): jnp.einsum('shp,uhp->hsu', x_block, grad_block, preferred_element_type=jn...  5.34 us
    unnamed x51, local copies, waits for them, and re-layouts  5.26 us
  transfers between devices with their start and end apart: 3, of which 2 were waited for; matrix products, arithmetic and copies ran while one was open for 15% of the time, Pallas kernels for 0%

commit v1 on v0

--- a/solution.py
+++ b/solution.py
@@ -121,8 +121,15 @@
         (jnp.transpose(received, (1, 0, 2)), gains),
         reverse=True,
     )
-    returned = lax.all_to_all(
-        jnp.transpose(exclusive, (1, 0, 2)), "seq", split_axis=1, concat_axis=1, tiled=True
+    local_array = jnp.transpose(exclusive, (1, 0, 2))
+    returned = jnp.concatenate(
+        lax.all_to_all(
+            jnp.stack(jnp.split(local_array, lax.psum(1, "seq"), 1), axis=0),
+            "seq",
+            split_axis=0,
+            concat_axis=0,
+        ),
+        axis=1,
     )
     incoming = returned.reshape(grad_total.shape)
     carried = incoming

time: 142 us -> 135 us (0.951)
  other arithmetic: 12.4 us -> 5.51 us
  local copies, waits for them, and re-layouts: 16.6 us -> 22.8 us
  waiting for transfers between devices: 14.6 us -> 9.19 us
    dynamic_update_slice x0 -> x16, local copies, waits for them, and re-layouts: none -> 6.85 us  [body(): lax.scan(backward_step, jnp.zeros_like(received[:, 0]), (jnp.transpose(re...]
    unnamed x51 -> x40, local copies, waits for them, and re-layouts: 5.26 us -> 11 us
    mul x8, local copies, waits for them, and re-layouts: 5.48 us -> 0.08 us  [backward_step(): return (grad_piece + gain_piece[:, None] * running, running)]
    dynamic_update_slice x8 -> x0, other arithmetic: 5.13 us -> none  [body(): lax.scan(backward_step, jnp.zeros_like(received[:, 0]), (jnp.transpose(re...]
    all_to_all x1, waiting for transfers between devices: 5.48 us -> 1.82 us  [body(): lax.all_to_all(jnp.stack(jnp.split(local_array, lax.psum(1, 'seq'), 1), a...]
    psum x1, waiting for transfers between devices: 9.15 us -> 7.36 us  [body(): grad_input_map = lax.psum(grad_b_list[0], 'head')]
    dot_general x1, matrix products: 1.76 us -> 0.18 us  [prepare(): jnp.dot(b_block, c_block.T, preferred_element_type=jnp.float32)]
  transfers between devices with their start and end apart: 3 -> 3, of which waited for: 2 -> 2; matrix products, arithmetic and copies ran while one was open for 15% -> 14% of each run, Pallas kernels for 0% -> 0%
where the time goes in v1:
time: 135 us
  blocking collectives  45.9 us (34%)
  matrix products  23.3 us (17%)
  local copies, waits for them, and re-layouts  22.8 us (17%)
  between operations  15.7 us (12%)
  starting transfers between devices  12 us (9%)
  waiting for transfers between devices  9.19 us (7%)
  other arithmetic  5.51 us (4%)
    unnamed x1, blocking collectives  26.1 us
    psum x1, blocking collectives, body(): grad_rate = -lax.psum(rate_total, 'seq')  19.8 us
    unnamed x40, local copies, waits for them, and re-layouts  11 us
    psum x1, waiting for transfers between devices, body(): grad_input_map = lax.psum(grad_b_list[0], 'head')  7.36 us
    all_to_all x1, starting transfers between devices, body(): lax.all_to_all(sliced, 'seq', split_axis=1, concat_axis=1, tiled=True)  7.31 us
    dynamic_update_slice x16, local copies, waits for them, and re-layouts, body(): lax.scan(backward_step, jnp.zeros_like(received[:, 0]), (jnp.transpose(re...  6.85 us
    dot_general x1, matrix products, prepare(): jnp.einsum('shp,uhp->hsu', x_block, grad_block, preferred_element_type=jn...  5.34 us
    dot_general x1, matrix products, prepare(): jnp.einsum('hsu,un->hsn', paired, c_block, preferred_element_type=jnp.flo...  5.05 us
  transfers between devices with their start and end apart: 3, of which 2 were waited for; matrix products, arithmetic and copies ran while one was open for 14% of the time, Pallas kernels for 0%

profile of v1, /device:TPU:0, one launch (start us, length us, event | category | flops | bytes accessed | tf_op | source)
XLA Modules:
  0.0 134.8 jit_solution(1520236713082113705)
XLA Ops:
  11.1 0.9 copy.54
  12.1 1.4 %copy.53 = bf16[256,1280]{0,1:T(8,128)(2,1)S(1)} copy(bf16[256,1280]{1,0:T(8,128)(2,1)} %param.15) | data formatting | bytes 1310720 | tf_op args[5]
  13.5 0.8 copy-done.2
  14.3 1.7 %fusion.30 = f32[20,64,128]{2,1,0:T(8,128)S(1)} fusion(bf16[256,20,64]{0,2,1:T(8,128)(2,1)S(1)} %bitcast.128, f32[256,128]{0,1:T(8,128)S(1)} %copy.54, f32[20,256]{1,0:T(8,128)S(1)} %get-tuple-element.155, f32[20]{0:T(128)S(1)} %broadcast_multiply_fusion.1), kind=kOutput, calls=%fused_computation.37 | convolution fusion | flops 504135680 | bytes 1462352 | tf_op jit(solution)/shard_map/hun,uhp->hpn/dot_general | solution.py:34
  16.2 1.3 copy.56
  17.4 7.3 %all-to-all-start = ((f32[20,8,1024]{2,0,1:T(8,128)}), f32[20,8,1024]{2,0,1:T(8,128)S(1)}, u32[]{:S(2)}, u32[]{:S(2)}) async-start(f32[20,8,1024]{2,0,1:T(8,128)} %copy.56), calls=%async_computation | async-start | bytes 1572864 | tf_op jit(solution)/shard_map/all_to_all | solution.py:116
  26.4 26.1 %all-reduce = f32[160]{0:T(256)S(1)} all-reduce(f32[160]{0:T(256)S(1)} %dynamic-update-slice), channel_id=2, replica_groups=mesh['seq'=8,'head'=4] {'seq'}, use_global_device_ids=true, to_apply=%add | all-reduce | flops 160 | bytes 1280
  54.1 7.9 %while.17 = (s32[]{:T(128)}, f32[20,1024]{1,0:T(8,128)S(1)}, f32[8,20,1024]{2,0,1:T(8,128)S(1)}, f32[8,20,1024]{2,1,0:T(8,128)S(1)}, f32[8,20]{1,0:T(8,128)S(1)}, /*index=5*/s32[]{:T(128)}, s32[]{:T(128)}, s32[]{:T(128)}) while((s32[]{:T(128)}, f32[20,1024]{1,0:T(8,128)S(1)}, f32[8,20,1024]{2,0,1:T(8,128)S(1)}, ...), condition=%wide.region_3.4_spmd.clone, body=%wide.region_2.3_spmd.clone.sunk | while | flops 61444 | bytes 655727 | solution.py:118
  54.3 0.8 dynamic_update_slice.12
  60.3 0.8 dynamic_update_slice.12
  61.3 0.8 dynamic_update_slice.12
  67.6 4.5 %all-to-all-start.1 = ((f32[8,20,1,1024]{3,2,1,0:T(1,128)}), f32[8,20,1,1024]{3,2,1,0:T(1,128)S(1)}, u32[]{:S(2)}, u32[]{:S(2)}) async-start(f32[8,20,1,1024]{3,2,1,0:T(1,128)} %fusion.37), calls=%async_computation.1 | async-start | bytes 1310720 | tf_op jit(solution)/shard_map/all_to_all | solution.py:126
  72.4 3.2 %multiply_reduce_fusion.1 = f32[20,256]{1,0:T(8,128)} fusion(bf16[256,20,64]{0,2,1:T(8,128)(2,1)} %bitcast.129, f32[256,128]{0,1:T(8,128)} %copy-done.7, f32[1,20,64,128]{3,2,1,0:T(8,128)} %param.16), kind=kOutput, calls=%fused_computation.16 | convolution fusion | flops 504622080 | bytes 1462272 | tf_op jit(solution)/shard_map/uhp,hpn->hun/dot_general | solution.py:35
  75.6 3.9 %fusion.20 = f32[256,20,64]{0,2,1:T(8,128)} fusion(bf16[256,20,64]{0,2,1:T(8,128)(2,1)} %bitcast.130, f32[256,256]{1,0:T(8,128)S(1)} %fusion.50, f32[20,256]{1,0:T(8,128)S(1)} %get-tuple-element.156, pred[256,256]{1,0:T(8,128)(4,1)S(1)} %fusion.36), kind=kOutput, calls=%fused_computation.28 | convolution fusion | flops 174325760 | bytes 2314240 | tf_op jit(solution)/shard_map/hsu,uhp->shp/dot_general | solution.py:24
  79.5 5.3 %multiply_reduce_fusion = (f32[20]{0:T(128)}, f32[20,256,256]{2,1,0:T(8,128)}) fusion(f32[20,256]{1,0:T(8,128)S(1)} %bitcast.134, f32[20,256]{1,0:T(8,128)S(1)} %copy-done.6, f32[256,256]{1,0:T(8,128)S(1)} %fusion.50, f32[20,256]{1,0:T(8,128)S(1)} %get-tuple-element.156, pred[256,256]{1,0:T(8,128)(4,1)S(1)} %fusion.36, ...), kind=kOutput, calls=%fused_computation.3 | convolution fusion | flops 179568624 | bytes 6942800 | tf_op jit(solution)/shard_map/shp,uhp->hsu/dot_general | solution.py:20
  84.9 1.8 %all-to-all-done.1 = f32[8,20,1,1024]{3,2,1,0:T(1,128)S(1)} async-done(((f32[8,20,1,1024]{3,2,1,0:T(1,128)}), f32[8,20,1,1024]{3,2,1,0:T(1,128)S(1)}, u32[]{:S(2)}, u32[]{:S(2)}) %all-to-all-start.1) | async-done | bytes 655392 | tf_op jit(solution)/shard_map/all_to_all | solution.py:126
  87.2 1.9 %fusion.8 = (f32[20,256]{1,0:T(8,128)S(1)}, f32[20,128,256]{1,2,0:T(8,128)S(1)}) fusion(f32[256,128]{1,0:T(8,128)S(1)} %convert_element_type.21, f32[20,64,128]{2,1,0:T(8,128)S(1)} %reshape_reshape.3, bf16[256,20,64]{0,2,1:T(8,128)(2,1)S(1)} %bitcast.116), kind=kOutput, calls=%fused_computation.15 | convolution fusion | flops 504622080 | bytes 4083712 | tf_op jit(solution)/shard_map/shp,hpn->hsn/dot_general | solution.py:61
  89.0 0.9 multiply_reduce_fusion.4
  90.0 5.0 %fusion.7 = f32[256,128]{1,0:T(8,128)} fusion(f32[20,128,256]{1,2,0:T(8,128)S(1)} %get-tuple-element.158, f32[20,256]{1,0:T(8,128)S(1)} %get-tuple-element.153, f32[20,256]{1,0:T(8,128)S(1)} %copy-done.6, f32[20,256,256]{2,1,0:T(8,128)} %get-tuple-element.160, f32[20,256]{1,0:T(8,128)S(1)} %get-tuple-element.156, pred[256,256]{1,0:T(8,128)(4,1)} %copy-done.8, ...), kind=kOutput, calls=%fused_computation.14 | convolution fusion | flops 344686592 | bytes 8187904 | tf_op jit(solution)/shard_map/hsu,un->hsn/dot_general | solution.py:25
  95.6 2.0 %fusion.24 = bf16[256,20,64]{0,2,1:T(8,128)(2,1)S(1)} fusion(f32[256,20,64]{0,2,1:T(8,128)} %fusion.20, f32[20,64,128]{2,1,0:T(8,128)S(1)} %reshape_reshape.3, f32[256,20]{0,1:T(8,128)S(1)} %get-tuple-element.154, f32[256,20]{0,1:T(8,128)S(1)} %bitcast.136, bf16[256,128]{1,0:T(8,128)(2,1)S(1)} %copy-done.4), kind=kOutput, calls=%fused_computation.33 | convolution fusion | flops 504627200 | bytes 2727936 | tf_op jit(solution)/shard_map/sn,hpn->shp/dot_general | solution.py:60
  97.6 19.8 %psum.15 = f32[20]{0:T(128)S(1)} all-reduce(f32[20]{0:T(128)S(1)} %multiply_add_fusion), channel_id=1, replica_groups=mesh['seq'=8,'head'=4] {'seq'}, use_global_device_ids=true, to_apply=%region_12.13 | all-reduce | flops 20 | bytes 160 | tf_op jit(solution)/shard_map/psum | solution.py:150
  117.4 1.1 copy.61
  119.0 7.4 %all-reduce.3.cloned.1.call-done = f32[256,128]{1,0:T(8,128)} async-done(((f32[256,128]{1,0:T(8,128)}), f32[256,128]{1,0:T(8,128)}) %all-reduce.3.cloned.1.call-update) | async-done | bytes 131088 | tf_op jit(solution)/shard_map/psum | solution.py:149
  126.4 1.6 %copy.102 = f32[256,128]{1,0:T(8,128)} copy(f32[256,128]{1,0:T(8,128)} %all-reduce.3.cloned.1.call-done) | data formatting | bytes 262144
  (97 shorter events, 18.4 us)
Async XLA Ops:
  7.2 17.6 %copy-start.11 = (u32[32]{0:T(128)S(1)}, u32[32]{0:T(128)}, u32[]{:S(2)}) copy-start(u32[32]{0:T(128)} %constant.57) | copy-start | bytes 388
  7.2 45.3 %copy-start.4 = (bf16[256,128]{1,0:T(8,128)(2,1)S(1)}, bf16[256,128]{1,0:T(8,128)(2,1)}, u32[]{:S(2)}) copy-start(bf16[256,128]{1,0:T(8,128)(2,1)} %param.13) | copy-start | bytes 196612
  7.2 45.4 %copy-start = (bf16[256,1280]{1,0:T(8,128)(2,1)S(1)}, bf16[256,1280]{1,0:T(8,128)(2,1)}, u32[]{:S(2)}) copy-start(bf16[256,1280]{1,0:T(8,128)(2,1)} %param.10) | copy-start | bytes 1966084
  7.2 45.6 %copy-start.1 = (f32[1,20,64,128]{3,2,1,0:T(8,128)S(1)}, f32[1,20,64,128]{3,2,1,0:T(8,128)}, u32[]{:S(2)}) copy-start(f32[1,20,64,128]{3,2,1,0:T(8,128)} %param.16) | copy-start | bytes 1966084
  8.6 17.7 %copy-start.9 = (f32[20]{0:T(128)}, f32[20]{0:T(128)S(1)}, u32[]{:S(2)}) copy-start(f32[20]{0:T(128)S(1)} %neg.7) | copy-start | bytes 244
  12.1 5.4 %copy-start.7 = (f32[256,128]{0,1:T(8,128)}, f32[256,128]{0,1:T(8,128)S(1)}, u32[]{:S(2)}) copy-start(f32[256,128]{0,1:T(8,128)S(1)} %copy.54) | copy-start | bytes 393220
  12.1 41.7 %copy-start.5 = (bf16[256,128]{1,0:T(8,128)(2,1)S(1)}, bf16[256,128]{1,0:T(8,128)(2,1)}, u32[]{:S(2)}) copy-start(bf16[256,128]{1,0:T(8,128)(2,1)} %param.14) | copy-start | bytes 196612
  13.5 0.8 copy-start.2
  17.4 36.6 %all-to-all-start = ((f32[20,8,1024]{2,0,1:T(8,128)}), f32[20,8,1024]{2,0,1:T(8,128)S(1)}, u32[]{:S(2)}, u32[]{:S(2)}) async-start(f32[20,8,1024]{2,0,1:T(8,128)} %copy.56), calls=%async_computation | async-start | bytes 1572864 | tf_op jit(solution)/shard_map/all_to_all | solution.py:116
  53.8 25.7 %copy-start.8 = (pred[256,256]{1,0:T(8,128)(4,1)}, pred[256,256]{1,0:T(8,128)(4,1)S(1)}, u32[]{:S(2)}) copy-start(pred[256,256]{1,0:T(8,128)(4,1)S(1)} %fusion.36) | copy-start | bytes 196612
  67.6 19.0 %all-to-all-start.1 = ((f32[8,20,1,1024]{3,2,1,0:T(1,128)}), f32[8,20,1,1024]{3,2,1,0:T(1,128)S(1)}, u32[]{:S(2)}, u32[]{:S(2)}) async-start(f32[8,20,1,1024]{3,2,1,0:T(1,128)} %fusion.37), calls=%async_computation.1 | async-start | bytes 1310720 | tf_op jit(solution)/shard_map/all_to_all | solution.py:126
  72.1 54.2 %all-reduce.3.cloned.1.call-start = ((), (), s32[]{:S(2)}) async-start(), calls=%async_computation.2 | async-start | bytes 262144 | tf_op jit(solution)/shard_map/psum | solution.py:149
  75.6 3.9 %copy-start.3 = (bf16[256,1280]{0,1:T(8,128)(2,1)S(1)}, bf16[256,1280]{0,1:T(8,128)(2,1)}, u32[]{:S(2)}) copy-start(bf16[256,1280]{0,1:T(8,128)(2,1)} %copy-done.2) | copy-start | bytes 1966084
  75.6 3.9 %copy-start.6 = (f32[20,256]{1,0:T(8,128)S(1)}, f32[20,256]{1,0:T(8,128)}, u32[]{:S(2)}) copy-start(f32[20,256]{1,0:T(8,128)} %param.11) | copy-start | bytes 61444
  90.0 5.6 %copy-start.10 = (f32[20]{0:T(128)S(1)}, f32[20]{0:T(128)}, u32[]{:S(2)}) copy-start(f32[20]{0:T(128)} %get-tuple-element.159) | copy-start | bytes 244
Sparse Core Ops, SparseCore 0:
  95.2 31.1 all-reduce.2
